TPU v7x, 32 devices: a whole 2x2x4 slice. The times are simulated.
32 devices in a mesh: rep: 2 (over x), exp: 2 (over core), tp: 8 (over z, y).
Axes of the slice: x: 2, y: 2, z: 4, core: 2. Of those that a mesh axis runs over, the one named last changes fastest.
Arguments:
- tokens: bfloat16 [1024, 4096], P(('rep', 'exp'), 'tp'), parts along dimension 0
- smooth_in: float32 [4096], P('tp'), may hold values from 0.5 to 2
- expert_ids: int32 [1024, 2], P(('rep', 'exp')), parts along dimension 0, may hold values from 0 to 3, as said below
- gate_fixed: int32 [1024, 2], P(('rep', 'exp')), parts along dimension 0, may hold values from 1 to 32767
- slots: int32 [1024, 2], P(('rep', 'exp')), parts along dimension 0, may hold values from 0 to 255, as said below
- w_gate: bfloat16 [4, 4096, 7168], P('exp', None, 'tp')
- w_up: bfloat16 [4, 4096, 7168], P('exp', None, 'tp')
- w_down: bfloat16 [4, 7168, 4096], P('exp', 'tp')
- gate_scale: float32 [4, 7168], P('exp', 'tp'), may hold values from 0.00010557433 to 0.0004222973
- up_scale: float32 [4, 7168], P('exp', 'tp'), may hold values from 0.00010557433 to 0.0004222973
- smooth_mid: float32 [4, 7168], P('exp', 'tp'), may hold values from 0.5 to 2
- down_scale: float32 [4, 4096], P('exp'), may hold values from 0.00015961338 to 0.0006384535
Outputs:
- moe_out: bfloat16 [1024, 4096], P(('rep', 'exp'), 'tp'), parts along dimension 0
There are 2 independent parts, one for each index of `rep`. A program takes and returns all parts, laid end to end along the dimension named above; an argument that names none is the same for every part. Nothing has to cross between parts.
Inputs may be any that keep to these rules, and one draw needn't show every extreme that they name: `expert_ids`: the two experts of a token differ. Within one aligned block of 256 tokens (the tokens of one index of exp), the slots of the pairs that name one expert are distinct and run from 0 to their number less one. In every block some expert is named by 192 or more tokens.
All inputs are finite; a program needn't handle non-finite values.
Results may differ from a plain program's by a relative error of at most 0.006.
Values may be sent and summed in bfloat16 or wider, within the bound.
A program may use at most 128 MiB of HBM per device.

v0:
```python
import jax
import jax.numpy as jnp
from jax import lax
from jax.sharding import PartitionSpec as P

CLIP_RATIO = 0.35
EPSILON = 1e-06


def per_device(
    tokens,
    smooth_in,
    expert_ids,
    gate_fixed,
    slots,
    w_gate,
    w_up,
    w_down,
    gate_scale,
    up_scale,
    smooth_mid,
    down_scale,
):
    n_groups = lax.axis_size("exp")
    local_experts = w_gate.shape[0]
    block_rows = tokens.shape[0]
    capacity = 3 * block_rows // 4
    rows_all = local_experts * n_groups * capacity
    smoothed = tokens.astype(jnp.float32) / smooth_in[None, :]
    local_peak = jnp.max(jnp.abs(smoothed), axis=1)
    row_peak_value = lax.pmax(local_peak, "tp")
    in_scale = CLIP_RATIO * (row_peak_value + EPSILON) / 127.0
    quantized = jnp.clip(smoothed / in_scale[:, None], -127.0, 127.0).astype(jnp.bfloat16)
    gate_values = gate_fixed.astype(jnp.float32)
    weight = gate_values / jnp.sum(gate_values, axis=1, keepdims=True)
    kept_pairs = slots < capacity
    target = expert_ids * capacity + jnp.minimum(slots, capacity - 1)
    positions = jnp.arange(rows_all, dtype=jnp.int32)
    place_first = (target[:, 0][None, :] == positions[:, None]) & kept_pairs[:, 0][None, :]
    place_second = (target[:, 1][None, :] == positions[:, None]) & kept_pairs[:, 1][None, :]
    placement_map = place_first | place_second
    send_rows = jnp.dot(
        placement_map.astype(jnp.bfloat16), quantized, preferred_element_type=jnp.float32
    ).astype(jnp.bfloat16)
    send_rows = send_rows.reshape(n_groups, local_experts, capacity, tokens.shape[1])
    scale_slots = jnp.sum(jnp.where(placement_map, in_scale[None, :], 0.0), axis=1).reshape(
        n_groups, local_experts, capacity
    )
    recv_rows = lax.all_to_all(send_rows, "exp", split_axis=0, concat_axis=0, tiled=True)
    recv_scale = lax.all_to_all(scale_slots, "exp", split_axis=0, concat_axis=0, tiled=True)
    arrived = lax.all_gather(recv_rows, "tp", axis=3, tiled=True)
    gate_more = jnp.einsum("secl,elf->secf", arrived, w_gate, preferred_element_type=jnp.float32)
    up_more = jnp.einsum("secl,elf->secf", arrived, w_up, preferred_element_type=jnp.float32)
    gate_pre = gate_more * recv_scale[..., None] * gate_scale[None, :, None, :]
    up_pre = up_more * recv_scale[..., None] * up_scale[None, :, None, :]
    hidden = jax.nn.silu(gate_pre) * up_pre / smooth_mid[None, :, None, :]
    hidden_max = lax.pmax(jnp.max(jnp.abs(hidden), axis=3), "tp")
    mid_scale = CLIP_RATIO * (hidden_max + EPSILON) / 127.0
    hidden_q = jnp.clip(hidden / mid_scale[..., None], -127.0, 127.0).astype(jnp.bfloat16)
    down_acc = jnp.einsum("secf,efd->secd", hidden_q, w_down, preferred_element_type=jnp.float32)
    partial_value = down_acc * mid_scale[..., None] * down_scale[None, :, None, :]
    summed = lax.psum_scatter(partial_value, "tp", scatter_dimension=3, tiled=True)
    returned = lax.all_to_all(summed, "exp", split_axis=0, concat_axis=0, tiled=True)
    slot_table = returned.reshape(rows_all, returned.shape[3])
    picked = jnp.take(slot_table, target, axis=0)
    pair_weight = jnp.where(kept_pairs, weight, 0.0)
    combined = jnp.sum(picked * pair_weight[:, :, None], axis=1)
    return combined.astype(jnp.bfloat16)


def solution(mesh):
    in_specs = (
        P(("rep", "exp"), "tp"),
        P("tp"),
        P(("rep", "exp"), None),
        P(("rep", "exp"), None),
        P(("rep", "exp"), None),
        P("exp", None, "tp"),
        P("exp", None, "tp"),
        P("exp", "tp", None),
        P("exp", "tp"),
        P("exp", "tp"),
        P("exp", "tp"),
        P("exp", None),
    )
    out_specs = P(("rep", "exp"), "tp")
    return jax.shard_map(
        per_device, mesh=mesh, in_specs=in_specs, out_specs=out_specs, check_vma=False
    )
```

profile of v0, /device:TPU:0, one launch (start us, length us, event | category | flops | bytes accessed | tf_op | source)
XLA Modules:
  0.0 419.6 jit_solution(16711710052682556564)
XLA Ops:
  6.5 0.0 all-gather.2.cloned.1.call-start
  6.5 0.7 compare_and_fusion
  7.3 0.7 convert_reduce_fusion
  8.0 0.7 divide_select_fusion
  8.7 1.1 fusion.24
  9.8 23.2 %pmax.14 = f32[256]{0:T(256)S(1)} all-reduce(f32[256]{0:T(256)S(1)} %fusion.24), channel_id=1, replica_groups=mesh['rep'=2,'exp'=2,'tp'=8] {'tp'}, use_global_device_ids=true, to_apply=%region_1.0 | all-reduce | flops 256 | bytes 2048 | tf_op jit(solution)/shard_map/pmax | solution.py:31
  33.0 1.5 convolution_convert_fusion
  34.5 4.4 %all_to_all.15 = bf16[2,2,192,512]{3,2,1,0:T(8,128)(2,1)S(1)} all-to-all(bf16[2,2,192,512]{3,2,1,0:T(8,128)(2,1)S(1)} %bitcast.44), channel_id=1, replica_groups=mesh['rep'=2,'exp'=2,'tp'=8] {'exp'}, dimensions={0} | all-to-all | bytes 1572864 | tf_op jit(solution)/shard_map/all_to_all | solution.py:49
  38.8 0.9 copy.29
  39.8 0.0 all-gather.2.cloned.1.call-update
  39.8 0.0 reduce-scatter.2.cloned.1.call-start
  39.8 0.3 select_reduce_fusion
  40.2 0.1 reshape.30
  40.3 3.7 all_to_all.16
  44.0 92.7 %all-gather.2.cloned.1.call-done = bf16[2,2,192,4096]{3,2,0,1:T(8,128)(2,1)} async-done(((bf16[2,2,192,512]{3,2,0,1:T(8,128)(2,1)}), bf16[2,2,192,4096]{3,2,0,1:T(8,128)(2,1)}) %all-gather.2.cloned.1.call-update) | async-done | bytes 6291472 | tf_op jit(solution)/shard_map/all_gather | solution.py:51
  136.7 14.6 %fusion.2 = f32[2,2,192,896]{3,2,1,0:T(8,128)S(1)} fusion(bf16[2,2,192,4096]{3,2,0,1:T(8,128)(2,1)} %all-gather.2.cloned.1.call-done, bf16[2,4096,896]{2,1,0:T(8,128)(2,1)} %param.18), kind=kOutput, calls=%fused_computation.3 | convolution fusion | flops 5637144576 | bytes 23724032 | tf_op jit(solution)/shard_map/secl,elf->secf/dot_general | solution.py:53
  151.3 0.0 copy-done.2
  151.3 0.0 copy-start.1
  151.3 10.8 %abs_reduce_fusion = (f32[2,2,192]{2,0,1:T(2,128)S(1)}, f32[2,2,192,896]{3,2,0,1:T(8,128)S(1)}) fusion(f32[2,896]{1,0:T(2,128)S(1)} %copy-done.4, f32[2,896]{1,0:T(2,128)S(1)} %copy-done.2, f32[2,2,192,896]{3,2,1,0:T(8,128)S(1)} %fusion.2, f32[2,896]{1,0:T(2,128)S(1)} %copy-done.3, f32[2,2,192]{2,0,1:T(2,128)S(1)} %copy.30, ...), kind=kOutput, calls=%fused_computation.15 | convolution fusion | flops 5645401088 | bytes 26504192 | tf_op jit(solution)/shard_map/secl,elf->secf/dot_general | solution.py:52
  162.2 18.8 %pmax.15 = f32[2,2,192]{2,0,1:T(2,128)S(1)} all-reduce(f32[2,2,192]{2,0,1:T(2,128)S(1)} %get-tuple-element.13), channel_id=1, replica_groups=mesh['rep'=2,'exp'=2,'tp'=8] {'tp'}, use_global_device_ids=true, to_apply=%region_4.5 | all-reduce | flops 768 | bytes 6144 | tf_op jit(solution)/shard_map/pmax | solution.py:57
  181.0 14.8 %fusion.6 = f32[2,2,192,4096]{3,2,0,1:T(8,128)} fusion(bf16[2,896,4096]{2,1,0:T(8,128)(2,1)} %param.19, f32[2,4096]{1,0:T(2,128)S(1)} %copy-done.1, f32[2,2,192]{2,0,1:T(2,128)S(1)} %add_multiply_fusion, f32[2,2,192,896]{3,2,0,1:T(8,128)S(1)} %get-tuple-element.14, f32[2,896]{1,0:T(2,128)S(1)} %copy-done.4), kind=kOutput, calls=%fused_computation.8 | convolution fusion | flops 5646188544 | bytes 30058496 | tf_op jit(solution)/shard_map/secf,efd->secd/dot_general | solution.py:60
  195.8 0.0 reduce-scatter.2.cloned.1.call-update
  195.8 0.1 copy.32
  196.0 0.1 reshape.34
  196.1 0.1 copy.33
  196.2 0.2 copy.28
  196.4 204.7 %reduce-scatter.2.cloned.1.call-done = f32[2,2,192,512]{3,2,0,1:T(8,128)} async-done(((f32[2,2,192,4096]{3,2,0,1:T(8,128)}), f32[2,2,192,512]{3,2,0,1:T(8,128)}) %reduce-scatter.2.cloned.1.call-update) | async-done | bytes 1572880 | tf_op jit(solution)/shard_map/reduce_scatter | solution.py:62
  401.1 1.5 copy.31
  402.6 5.0 %all_to_all.17 = f32[2,2,192,512]{3,2,1,0:T(8,128)S(1)} all-to-all(f32[2,2,192,512]{3,2,1,0:T(8,128)S(1)} %copy.31), channel_id=1, replica_groups=mesh['rep'=2,'exp'=2,'tp'=8] {'exp'}, dimensions={0} | all-to-all | bytes 3145728 | tf_op jit(solution)/shard_map/all_to_all | solution.py:63
  407.6 1.6 gather_fusion
  409.3 0.6 reshape.33
  409.9 2.9 multiply_reduce_fusion
  (15 shorter events, 0.1 us)
Async XLA Ops:
  6.5 130.1 %all-gather.2.cloned.1.call-start = ((), (), s32[]{:S(2)}) async-start(), calls=%async_computation.4 | async-start | bytes 7077888 | tf_op jit(solution)/shard_map/all_gather | solution.py:51
  39.8 361.3 %reduce-scatter.2.cloned.1.call-start = ((), (), s32[]{:S(2)}) async-start(), calls=%async_computation.5 | async-start | bytes 14155776 | tf_op jit(solution)/shard_map/reduce_scatter | solution.py:62
  43.9 107.3 %copy-start.2 = (f32[2,896]{1,0:T(2,128)S(1)}, f32[2,896]{1,0:T(2,128)}, u32[]{:S(2)}) copy-start(f32[2,896]{1,0:T(2,128)} %param.21) | copy-start | bytes 21508
  43.9 107.4 %copy-start.3 = (f32[2,896]{1,0:T(2,128)S(1)}, f32[2,896]{1,0:T(2,128)}, u32[]{:S(2)}) copy-start(f32[2,896]{1,0:T(2,128)} %param.20) | copy-start | bytes 21508
  44.0 107.4 %copy-start.4 = (f32[2,896]{1,0:T(2,128)S(1)}, f32[2,896]{1,0:T(2,128)}, u32[]{:S(2)}) copy-start(f32[2,896]{1,0:T(2,128)} %param.22) | copy-start | bytes 21508
  136.7 14.6 %copy-start = (bf16[2,2,192,4096]{3,2,0,1:T(8,128)(2,1)S(1)}, bf16[2,2,192,4096]{3,2,0,1:T(8,128)(2,1)}, u32[]{:S(2)}) copy-start(bf16[2,2,192,4096]{3,2,0,1:T(8,128)(2,1)} %all-gather.2.cloned.1.call-done) | copy-start | bytes 18874372
  151.3 29.6 %copy-start.1 = (f32[2,4096]{1,0:T(2,128)S(1)}, f32[2,4096]{1,0:T(2,128)}, u32[]{:S(2)}) copy-start(f32[2,4096]{1,0:T(2,128)} %param.23) | copy-start | bytes 98308
Sparse Core Ops, SparseCore 0:
  39.9 96.7 all-gather.1
  195.9 205.1 reduce-scatter.1
where the time goes:
time: 420 us
  waiting for transfers between devices  297 us (71%)
  blocking collectives  55 us (13%)
  matrix products  41.7 us (10%)
  between operations  13.6 us (3%)
  other arithmetic  6.44 us (2%)
  local copies, waits for them, and re-layouts  5.43 us (1%)
    reduce_scatter x1, waiting for transfers between devices, per_device(): lax.psum_scatter(partial_value, 'tp', scatter_dimension=3, tiled=True)  205 us
    all_gather x1, waiting for transfers between devices, per_device(): arrived = lax.all_gather(recv_rows, 'tp', axis=3, tiled=True)  92.7 us
    pmax x1, blocking collectives, per_device(): row_peak_value = lax.pmax(local_peak, 'tp')  23.2 us
    pmax x1, blocking collectives, per_device(): hidden_max = lax.pmax(jnp.max(jnp.abs(hidden), axis=3), 'tp')  18.8 us
    dot_general x1, matrix products, per_device(): jnp.einsum('secf,efd->secd', hidden_q, w_down, preferred_element_type=jnp...  14.8 us
    dot_general x1, matrix products, per_device(): jnp.einsum('secl,elf->secf', arrived, w_up, preferred_element_type=jnp.fl...  14.6 us
    dot_general x1, matrix products, per_device(): jnp.einsum('secl,elf->secf', arrived, w_gate, preferred_element_type=jnp....  10.8 us
  transfers between devices with their start and end apart: 2, of which 2 were waited for; matrix products, arithmetic and copies ran while one was open for 0% of the time, Pallas kernels for 0%

commit v1 on v0

--- a/solution.py
+++ b/solution.py
@@ -48,7 +48,7 @@
     )
     recv_rows = lax.all_to_all(send_rows, "exp", split_axis=0, concat_axis=0, tiled=True)
     recv_scale = lax.all_to_all(scale_slots, "exp", split_axis=0, concat_axis=0, tiled=True)
-    arrived = lax.all_gather(recv_rows, "tp", axis=3, tiled=True)
+    arrived = jnp.concatenate(lax.all_gather(recv_rows, "tp"), axis=3)
     gate_more = jnp.einsum("secl,elf->secf", arrived, w_gate, preferred_element_type=jnp.float32)
     up_more = jnp.einsum("secl,elf->secf", arrived, w_up, preferred_element_type=jnp.float32)
     gate_pre = gate_more * recv_scale[..., None] * gate_scale[None, :, None, :]

time: 420 us -> 439 us (1.045)
  local copies, waits for them, and re-layouts: 5.43 us -> 23.9 us
    reshape x0 -> x1, local copies, waits for them, and re-layouts: none -> 10.4 us  [per_device(): arrived = jnp.concatenate(lax.all_gather(recv_rows, 'tp'), axis=3)]
    all_gather x0 -> x1, local copies, waits for them, and re-layouts: none -> 9.02 us  [per_device(): arrived = jnp.concatenate(lax.all_gather(recv_rows, 'tp'), axis=3)]
where the time goes in v1:
time: 439 us; the launch traced here: 438 us
  waiting for transfers between devices  297 us (68%)
  blocking collectives  55.7 us (13%)
  matrix products  41.8 us (10%)
  local copies, waits for them, and re-layouts  23.9 us (5%)
  between operations  13.6 us (3%)
  other arithmetic  6.44 us (1%)
    reduce_scatter x1, waiting for transfers between devices, per_device(): lax.psum_scatter(partial_value, 'tp', scatter_dimension=3, tiled=True)  205 us
    all_gather x1, waiting for transfers between devices, per_device(): arrived = jnp.concatenate(lax.all_gather(recv_rows, 'tp'), axis=3)  91.9 us
    pmax x1, blocking collectives, per_device(): row_peak_value = lax.pmax(local_peak, 'tp')  23.2 us
    pmax x1, blocking collectives, per_device(): hidden_max = lax.pmax(jnp.max(jnp.abs(hidden), axis=3), 'tp')  18.7 us
    dot_general x1, matrix products, per_device(): jnp.einsum('secf,efd->secd', hidden_q, w_down, preferred_element_type=jnp...  14.8 us
    dot_general x1, matrix products, per_device(): jnp.einsum('secl,elf->secf', arrived, w_up, preferred_element_type=jnp.fl...  14.6 us
    dot_general x1, matrix products, per_device(): jnp.einsum('secl,elf->secf', arrived, w_gate, preferred_element_type=jnp....  10.8 us
    reshape x1, local copies, waits for them, and re-layouts, per_device(): arrived = jnp.concatenate(lax.all_gather(recv_rows, 'tp'), axis=3)  10.4 us
  transfers between devices with their start and end apart: 2, of which 2 were waited for; matrix products, arithmetic and copies ran while one was open for 0% of the time, Pallas kernels for 0%

profile of v1, /device:TPU:0, one launch (start us, length us, event | category | flops | bytes accessed | tf_op | source)
XLA Modules:
  0.0 438.1 jit_solution(9500382347376542037)
XLA Ops:
  6.5 0.0 all-gather.3.cloned.1.call-start
  6.5 0.7 compare_and_fusion
  7.3 0.7 convert_reduce_fusion
  8.0 0.7 divide_select_fusion
  8.7 1.1 fusion.24
  9.8 23.2 %pmax.14 = f32[256]{0:T(256)S(1)} all-reduce(f32[256]{0:T(256)S(1)} %fusion.24), channel_id=1, replica_groups=mesh['rep'=2,'exp'=2,'tp'=8] {'tp'}, use_global_device_ids=true, to_apply=%region_1.0 | all-reduce | flops 256 | bytes 2048 | tf_op jit(solution)/shard_map/pmax | solution.py:31
  33.0 1.5 convolution_convert_fusion
  34.5 5.2 %all_to_all.15 = bf16[2,2,192,512]{3,2,1,0:T(8,128)(2,1)} all-to-all(bf16[2,2,192,512]{3,2,1,0:T(8,128)(2,1)S(1)} %bitcast.54), channel_id=1, replica_groups=mesh['rep'=2,'exp'=2,'tp'=8] {'exp'}, dimensions={0} | all-to-all | bytes 1572864 | tf_op jit(solution)/shard_map/all_to_all | solution.py:49
  39.6 0.0 all-gather.3.cloned.1.call-update
  39.6 0.0 reduce-scatter.2.cloned.1.call-start
  39.7 0.3 select_reduce_fusion
  40.0 0.1 reshape.38
  40.1 3.7 all_to_all.16
  43.8 91.9 %all-gather.3.cloned.1.call-done = bf16[16,2,192,512]{3,2,1,0:T(8,128)(2,1)} async-done(((bf16[2,2,192,512]{3,2,1,0:T(8,128)(2,1)}), bf16[16,2,192,512]{3,2,1,0:T(8,128)(2,1)}) %all-gather.3.cloned.1.call-update) | async-done | bytes 6291472 | tf_op jit(solution)/shard_map/all_gather | solution.py:51
  135.7 9.0 %copy.38 = bf16[8,2,2,192,512]{4,0,3,1,2:T(8,128)(2,1)} copy(bf16[8,2,2,192,512]{4,3,2,1,0:T(8,128)(2,1)} %bitcast.53) | data formatting | bytes 12582912 | tf_op jit(solution)/shard_map/all_gather | solution.py:51
  144.8 10.4 %reshape.37 = bf16[2,2,192,4096]{3,2,0,1:T(8,128)(2,1)} reshape(bf16[2,2,192,8,512]{4,3,2,0,1:T(8,128)(2,1)} %bitcast.52) | data formatting | bytes 12582912 | tf_op jit(solution)/shard_map/reshape | solution.py:51
  155.2 14.6 %fusion.2 = f32[2,2,192,896]{3,2,1,0:T(8,128)S(1)} fusion(bf16[2,2,192,4096]{3,2,0,1:T(8,128)(2,1)} %reshape.37, bf16[2,4096,896]{2,1,0:T(8,128)(2,1)} %param.18), kind=kOutput, calls=%fused_computation.3 | convolution fusion | flops 5637144576 | bytes 23724032 | tf_op jit(solution)/shard_map/secl,elf->secf/dot_general | solution.py:53
  169.9 0.0 copy-start.1
  169.9 10.8 %abs_reduce_fusion = (f32[2,2,192]{2,0,1:T(2,128)S(1)}, f32[2,2,192,896]{3,2,0,1:T(8,128)S(1)}) fusion(f32[2,896]{1,0:T(2,128)S(1)} %copy-done.4, f32[2,896]{1,0:T(2,128)S(1)} %copy-done.2, f32[2,2,192,896]{3,2,1,0:T(8,128)S(1)} %fusion.2, f32[2,896]{1,0:T(2,128)S(1)} %copy-done.3, f32[2,2,192]{2,0,1:T(2,128)S(1)} %copy.30, ...), kind=kOutput, calls=%fused_computation.16 | convolution fusion | flops 5645401088 | bytes 26504192 | tf_op jit(solution)/shard_map/secl,elf->secf/dot_general | solution.py:52
  180.7 18.7 %pmax.15 = f32[2,2,192]{2,0,1:T(2,128)S(1)} all-reduce(f32[2,2,192]{2,0,1:T(2,128)S(1)} %get-tuple-element.13), channel_id=1, replica_groups=mesh['rep'=2,'exp'=2,'tp'=8] {'tp'}, use_global_device_ids=true, to_apply=%region_4.5 | all-reduce | flops 768 | bytes 6144 | tf_op jit(solution)/shard_map/pmax | solution.py:57
  199.5 14.8 %fusion.6 = f32[2,2,192,4096]{3,2,0,1:T(8,128)} fusion(bf16[2,896,4096]{2,1,0:T(8,128)(2,1)} %param.19, f32[2,4096]{1,0:T(2,128)S(1)} %copy-done.1, f32[2,2,192]{2,0,1:T(2,128)S(1)} %add_multiply_fusion, f32[2,2,192,896]{3,2,0,1:T(8,128)S(1)} %get-tuple-element.14, f32[2,896]{1,0:T(2,128)S(1)} %copy-done.4), kind=kOutput, calls=%fused_computation.8 | convolution fusion | flops 5646188544 | bytes 30058496 | tf_op jit(solution)/shard_map/secf,efd->secd/dot_general | solution.py:60
  214.3 0.0 reduce-scatter.2.cloned.1.call-update
  214.3 0.1 copy.32
  214.5 0.1 reshape.42
  214.6 0.1 copy.33
  214.8 0.2 copy.28
  215.0 204.6 %reduce-scatter.2.cloned.1.call-done = f32[2,2,192,512]{3,2,0,1:T(8,128)} async-done(((f32[2,2,192,4096]{3,2,0,1:T(8,128)}), f32[2,2,192,512]{3,2,0,1:T(8,128)}) %reduce-scatter.2.cloned.1.call-update) | async-done | bytes 1572880 | tf_op jit(solution)/shard_map/reduce_scatter | solution.py:62
  419.6 1.5 copy.31
  421.1 5.0 %all_to_all.17 = f32[2,2,192,512]{3,2,1,0:T(8,128)S(1)} all-to-all(f32[2,2,192,512]{3,2,1,0:T(8,128)S(1)} %copy.31), channel_id=1, replica_groups=mesh['rep'=2,'exp'=2,'tp'=8] {'exp'}, dimensions={0} | all-to-all | bytes 3145728 | tf_op jit(solution)/shard_map/all_to_all | solution.py:63
  426.1 1.6 gather_fusion
  427.7 0.6 reshape.41
  428.3 2.9 multiply_reduce_fusion
  (16 shorter events, 0.1 us)
Async XLA Ops:
  6.5 129.2 %all-gather.3.cloned.1.call-start = ((), (), s32[]{:S(2)}) async-start(), calls=%async_computation.5 | async-start | bytes 7077888 | tf_op jit(solution)/shard_map/all_gather | solution.py:51
  39.6 379.9 %reduce-scatter.2.cloned.1.call-start = ((), (), s32[]{:S(2)}) async-start(), calls=%async_computation.4 | async-start | bytes 14155776 | tf_op jit(solution)/shard_map/reduce_scatter | solution.py:62
  155.2 14.6 %copy-start = (bf16[2,2,192,4096]{3,2,0,1:T(8,128)(2,1)S(1)}, bf16[2,2,192,4096]{3,2,0,1:T(8,128)(2,1)}, u32[]{:S(2)}) copy-start(bf16[2,2,192,4096]{3,2,0,1:T(8,128)(2,1)} %reshape.37) | copy-start | bytes 18874372
  155.2 14.6 %copy-start.2 = (f32[2,896]{1,0:T(2,128)S(1)}, f32[2,896]{1,0:T(2,128)}, u32[]{:S(2)}) copy-start(f32[2,896]{1,0:T(2,128)} %param.21) | copy-start | bytes 21508
  155.2 14.7 %copy-start.3 = (f32[2,896]{1,0:T(2,128)S(1)}, f32[2,896]{1,0:T(2,128)}, u32[]{:S(2)}) copy-start(f32[2,896]{1,0:T(2,128)} %param.20) | copy-start | bytes 21508
  155.2 14.7 %copy-start.4 = (f32[2,896]{1,0:T(2,128)S(1)}, f32[2,896]{1,0:T(2,128)}, u32[]{:S(2)}) copy-start(f32[2,896]{1,0:T(2,128)} %param.22) | copy-start | bytes 21508
  169.9 29.6 %copy-start.1 = (f32[2,4096]{1,0:T(2,128)S(1)}, f32[2,4096]{1,0:T(2,128)}, u32[]{:S(2)}) copy-start(f32[2,4096]{1,0:T(2,128)} %param.23) | copy-start | bytes 98308
Sparse Core Ops, SparseCore 0:
  39.8 95.9 all-gather.2
  214.5 205.0 reduce-scatter.1
